TPU v7x, 32 devices: a whole 2x2x4 slice. The times are simulated.
32 devices in a mesh: groups: 2 (over x), tile: 16 (over z, y, core).
Axes of the slice: x: 2, y: 2, z: 4, core: 2. Of those that a mesh axis runs over, the one named last changes fastest.
Arguments:
- tracer: float32 [32, 6, 8, 128, 128], P(('groups', 'tile')), parts along dimension 0, may hold values from -6 to 6
- courant_east: bfloat16 [32, 6, 8, 128, 128], P(('groups', 'tile')), parts along dimension 0, may hold values from -1.5 to 1.5
- courant_north: bfloat16 [32, 6, 8, 128, 128], P(('groups', 'tile')), parts along dimension 0, may hold values from -1.5 to 1.5
- diffusivity: bfloat16 [32, 6, 8, 128, 128], P(('groups', 'tile')), parts along dimension 0, may hold values from 0.049804688 to 5
- seam_table: int32 [6, 4, 3], replicated, may hold values from 0 to 5, as said below
Outputs:
- updated: float32 [32, 6, 8, 128, 128], P(('groups', 'tile')), parts along dimension 0
There are 2 independent parts, one for each index of `groups`. A program takes and returns all parts, laid end to end along the dimension named above; an argument that names none is the same for every part. Nothing has to cross between parts.
Inputs may be any that keep to these rules, and one draw needn't show every extreme that they name: seam_table[p, e] = (q, f, r) names the edge f of panel q != p that borders edge e of panel p, and r is 1 where their edge indices run in opposite directions, 0 otherwise; the 24 edges form 12 pairs whose entries name each other with the same r, as on the faces of a cube ; edge 3 of panel 0 borders edge 3 of panel 1.
All inputs are finite; a program needn't handle non-finite values.
Results may differ from a plain program's by a relative error of at most 0.0003.
Values sent between devices are 32-bit elements; how exact they have to be, the bound alone decides.
A program may use at most 128 MiB of HBM per device.

v0:
```python
import functools
import math

import jax
import jax.numpy as jnp
from jax import lax
from jax.experimental import pallas as pl
from jax.experimental.pallas import tpu as pltpu
from jax.sharding import PartitionSpec as P

DEPTH = 2
HUBS = 4
VMEM_LIMIT = 59 * 1024 * 1024


def tile_of(device, parity, total):
    return lax.rem(device + total - parity * (total // 2 + 1) + total, total)


def edge_state(device, parity, total, across):
    tile = tile_of(device, parity, total)
    row, col = tile // across, lax.rem(tile, across)
    on = (col == 0, row == across - 1, col == across - 1, row == 0)
    return on, (row, col, row, col)


def edge_tile(edge, spot, across):
    return (spot * across, (across - 1) * across + spot, spot * across + across - 1, spot)[edge]


def central(q, p, k, start, size):
    ct = q.shape[2]
    mid = q[p, k, start:start + size]
    none = jnp.zeros((DEPTH, 128), jnp.float32)
    if start == 0:
        ext = jnp.concatenate([none, q[p, k, 0:size + DEPTH]], axis=0)
        near = [ext[o:o + size] for o in (0, 1, 3, 4)]
    elif start + size == ct:
        ext = jnp.concatenate([q[p, k, start - DEPTH:ct], none], axis=0)
        near = [ext[o:o + size] for o in (0, 1, 3, 4)]
    else:
        near = [q[p, k, start + o:start + o + size] for o in (-2, -1, 1, 2)]
    along_i = 8.0 * (near[2] - near[1]) - (near[3] - near[0])
    along_j = 8.0 * (pltpu.roll(mid, 127, 1) - pltpu.roll(mid, 1, 1)) - (
        pltpu.roll(mid, 126, 1) - pltpu.roll(mid, 2, 1))
    return mid, along_i, along_j


def factors(coupling, levels):
    inverses, ratios, below = [], [], None
    for k in range(levels):
        here = coupling(k)
        if k == 0:
            inverse = 1.0 / (1.0 + here)
        else:
            inverse = 1.0 / ((1.0 + here) + below * (1.0 - ratios[-1]))
        inverses.append(inverse)
        ratios.append(here * inverse)
        below = here
    return inverses, ratios


def solve(forced, coupling, levels):
    ratios, partials = [], []
    for k in range(levels):
        value, here = forced(k), coupling(k)
        if k == 0:
            inverse = 1.0 / (1.0 + here)
            current = value * inverse
        else:
            inverse = 1.0 / ((1.0 + here) + below * (1.0 - ratios[-1]))
            current = (value + below * partials[-1]) * inverse
        ratios.append(here * inverse)
        partials.append(current)
        below = here
    solved = [partials[-1]]
    for k in range(levels - 2, -1, -1):
        solved.insert(0, partials[k] + ratios[k] * solved[0])
    return solved


def update_panel(q, east, north, coupling, u, p):
    _, levels, ct, _ = q.shape
    size = 16
    for start in range(0, ct, size):
        part = pl.ds(start, size)

        def forced(k):
            mid, along_i, along_j = central(q, p, k, start, size)
            return mid - (east[p, k, part].astype(jnp.float32) * along_i
                          + north[p, k, part].astype(jnp.float32) * along_j) * (1.0 / 12.0)

        solved = solve(forced, lambda k: coupling[p, k, part].astype(jnp.float32), levels)
        for k in range(levels):
            u[p, k, part] = solved[k]


def gather_columns(field, p, n, gathered):
    _, levels, ct, _ = field.shape
    lane_group = lax.broadcasted_iota(jnp.int32, (ct, 128), 1) // 4
    for k in range(levels):
        group = n * levels + k
        turned = pltpu.roll(field[p, k].astype(jnp.float32), (group * 4 + DEPTH) % 128, 1)
        gathered = jnp.where(lane_group == group, turned, gathered)
    return gathered


def columns_of(field, parity, half):
    gathered = jnp.zeros((field.shape[2], 128), jnp.float32)
    for n in range(half):
        gathered = gather_columns(field, 2 * n + parity, n, gathered)
    return gathered.T


def packed_columns(upright, group):
    pair = upright[(group // 2) * 8:(group // 2) * 8 + 8]
    return pltpu.roll(pair, 2 if group % 2 == 0 else 6, 0)


def packed_rows(field, p, k, low):
    ct = field.shape[2]
    top = field[p, k, 0:16].astype(jnp.float32)[0:8]
    bottom = field[p, k, ct - 16:ct].astype(jnp.float32)[8:16]
    return jnp.where(low, top, bottom)


def exchange_kernel(total, across, table_in, tracer, east_in, north_in, coupling_in, u, cols, rows,
                    table, q, east, north, coupling, s, r, d, h, own, drive, carry, ratio, still, ghost, change,
                    t_sem, q_sem, c_sem, send1, r_sem, send2, h_sem, peer, ready):
    panels, levels, ct, _ = q.shape
    half = panels // 2
    per = DEPTH * levels // HUBS
    first_hub = total // 2 - HUBS + 1
    me = lax.axis_index("tile")
    steps = (total - 1, across, 1, total - across)
    offsets = sorted(set(steps))

    def hub_flag(device):
        ahead = device - first_hub
        inside = jnp.logical_and(ahead >= 0, ahead < 2 * HUBS)
        return jnp.where(jnp.logical_and(inside, lax.rem(ahead + total, 2) == 0), 1, 0)

    am_hub = hub_flag(me)

    def load(p):
        return pltpu.make_async_copy(tracer.at[p], q.at[p], q_sem.at[p])

    fields = ((east_in, east), (north_in, north), (coupling_in, coupling))

    def loads(p):
        return [pltpu.make_async_copy(src.at[p], dst.at[p], c_sem.at[i, p]) for i, (src, dst) in enumerate(fields)]

    for parity in range(2):
        for n in range(half):
            load(2 * n + parity).start()
    fetch = pltpu.make_async_copy(table_in, table, t_sem)
    fetch.start()

    barrier = pltpu.get_barrier_semaphore()

    def signal(semaphore, device):
        pl.semaphore_signal(semaphore, inc=1, device_id={"tile": device}, device_id_type=pl.DeviceIdType.MESH)

    @pl.when(am_hub == 1)
    def _():
        def greet(i, carry):
            signal(barrier, lax.rem(me + i, total))
            return carry

        lax.fori_loop(1, total, greet, 0)

    @pl.when(am_hub == 0)
    def _():
        for offset in offsets:
            other = lax.rem(me + offset, total)

            @pl.when(other > me)
            def _():
                signal(barrier, other)

    expected, peers = HUBS - am_hub, 0
    for offset in offsets:
        other = lax.rem(me + offset, total)
        plain = 1 - hub_flag(other)
        expected = expected + jnp.where(other < me, plain, 0)
        peers = peers + jnp.where(other > me, plain, 0)

    def remote(src, dst, send, recv, device):
        return pltpu.make_async_remote_copy(
            src_ref=src, dst_ref=dst, send_sem=send, recv_sem=recv,
            device_id={"tile": device}, device_id_type=pl.DeviceIdType.MESH)

    flat = q.reshape(panels * levels * ct, 128)
    blocks = levels // per
    for parity in range(2):
        gathered = jnp.zeros((ct, 128), jnp.float32)
        for n in range(half):
            p = 2 * n + parity
            load(p).wait()
            gathered = gather_columns(q, p, n, gathered)
            for block in range(blocks):
                for depth in range(DEPTH):
                    x, base = depth * blocks + block, (p * levels + block * per) * ct
                    s[parity, 3, n, x] = flat[pl.ds(base + depth, per, stride=ct)]
                    s[parity, 1, n, x] = flat[pl.ds(base + ct - 1 - depth, per, stride=ct)]
        own[parity] = gathered.T
        for n in range(half):
            for block in range(blocks):
                base = (n * levels + block * per) * 4
                for c, (e, depth) in enumerate(((2, 1), (2, 0), (0, 0), (0, 1))):
                    s[parity, e, n, depth * blocks + block] = own[parity, pl.ds(base + c, per, stride=4)]
        if parity == 0:
            for n in range(half):
                for copy in loads(n):
                    copy.start()
            pl.semaphore_wait(barrier, expected)
        on, along = edge_state(me, parity, total, across)
        for e in range(4):
            @pl.when(on[e])
            def _():
                slot = ((parity * 4 + e) * across + along[e]) * half

                def spread(i, carry):
                    hub = first_hub + 2 * i
                    src, dst = s.at[parity, e, :, i], r.at[pl.ds(slot, half)]

                    @pl.when(hub != me)
                    def _():
                        remote(src, dst, send1.at[parity, e], r_sem, hub).start()

                    @pl.when(hub == me)
                    def _():
                        pltpu.make_async_copy(src, dst, r_sem).start()

                    return carry

                lax.fori_loop(0, HUBS, spread, 0)

    for n in range(half, panels):
        for copy in loads(n):
            copy.start()

    @pl.when(am_hub == 0)
    def _():
        for offset in offsets:
            other = lax.rem(me + offset, total)

            @pl.when(other < me)
            def _():
                signal(peer, other)

    for i in range(HUBS):
        @pl.when(me != first_hub + 2 * i)
        def _():
            signal(ready, first_hub + 2 * i)

    @pl.when(peers > 0)
    def _():
        pl.semaphore_wait(peer, peers)

    for parity in range(2):
        on, _ = edge_state(me, parity, total, across)
        for e in range(4):
            @pl.when(jnp.logical_not(on[e]))
            def _():
                far = (e + 2) % 4
                remote(s.at[parity, e], h.at[parity, far], send1.at[parity, e],
                       h_sem.at[parity, far], lax.rem(me + steps[e], total)).start()

    def compute(first, last):
        def one(p, carry):
            for copy in loads(p):
                copy.wait()
            update_panel(q, east, north, coupling, u, p)
            return carry

        lax.fori_loop(first, last, one, 0)

    compute(0, half)
    fetch.wait()

    @pl.when(am_hub == 1)
    def _():
        pl.semaphore_wait(ready, total - 1)
        pltpu.make_async_copy(r, r, r_sem).wait()
        seams = [(edge_tile(e, spot, across) + parity * (total // 2 + 1), parity, e, spot)
                 for parity in range(2) for e in range(4) for spot in range(across)]
        for owner, parity, e, spot in sorted((tile % total, *rest) for tile, *rest in seams):
            slot = ((parity * 4 + e) * across + spot) * half
            for n in range(half):
                p = 2 * n + parity
                other, f, turn = table[0, e, p], table[1, e, p], table[2, e, p]
                base = (lax.rem(other, 2) * 4 + f) * across * half + other // 2
                place = jnp.where(turn == 1, across - 1 - spot, spot)
                d[slot + n] = r[base + place * half]
            src = d.at[pl.ds(slot, half)]
            dst = h.at[parity, e, :, (me - first_hub) // 2]

            @pl.when(me != owner)
            def _():
                remote(src, dst, send2.at[parity, e], h_sem.at[parity, e], owner).start()

            @pl.when(me == owner)
            def _():
                pltpu.make_async_copy(src, dst, h_sem.at[parity, e]).start()

    compute(half, panels)

    sub = lax.broadcasted_iota(jnp.int32, (8, 128), 0)
    low, inner = sub < 4, jnp.logical_and(sub >= 2, sub < 6)
    for parity in range(2):
        north_columns = columns_of(north, parity, half)
        coupling_columns = columns_of(coupling, parity, half)
        for n in range(half):
            p = 2 * n + parity
            inverses, ratios = factors(
                lambda k: jnp.where(inner, packed_columns(coupling_columns, n * levels + k),
                                    packed_rows(coupling, p, k, low)), levels)
            for k in range(levels):
                group = n * levels + k
                coef = jnp.where(inner, packed_columns(north_columns, group), packed_rows(east, p, k, low))
                scaled = coef * inverses[k] * (-1.0 / 12.0)
                mine = packed_columns(own[parity, (group // 2) * 8:(group // 2) * 8 + 8], group % 2)
                back1, back2 = pltpu.roll(mine, 7, 0), pltpu.roll(mine, 6, 0)
                fore1, fore2 = pltpu.roll(mine, 1, 0), pltpu.roll(mine, 2, 0)
                part = jnp.where(sub == 2, back2, jnp.where(sub == 3, back2 - 8.0 * back1,
                                 jnp.where(sub == 4, 8.0 * fore1 - fore2, -fore2)))
                spot = parity * half * levels + group
                drive[spot] = scaled
                still[spot] = jnp.where(inner, part * scaled, 0.0)
                ratio[spot] = ratios[k]
                if k > 0:
                    carry[spot] = inverses[k] * below
                below = jnp.where(inner, packed_columns(coupling_columns, group), packed_rows(coupling, p, k, low))

    lane = lax.broadcasted_iota(jnp.int32, (levels, 128), 1)
    change[...] = jnp.zeros_like(change)
    for parity in range(2):
        on, _ = edge_state(me, parity, total, across)
        for e in range(4):
            pltpu.make_async_copy(h.at[parity, e], h.at[parity, e], h_sem.at[parity, e]).wait()
        for n in range(half):
            p = 2 * n + parity
            first = (parity * half + n) * levels * 8

            def ghosts(e):
                turned = jnp.logical_and(on[e], table[2, e, p] == 1)
                found = []
                for depth in range(DEPTH):
                    rows_in = jnp.concatenate([h[parity, e, n, depth * blocks + block] for block in range(blocks)], axis=0)
                    found.append(jnp.where(turned, jnp.take_along_axis(rows_in, 127 - lane, axis=1), rows_in))
                return found

            south, east_side, north_side, west = (ghosts(e) for e in range(4))
            for spots, (above1, above2), (below1, below2) in (
                    ((2, 3, 4, 5), north_side, south), ((6, 7, 0, 1), east_side, west)):
                values = (-above1, 8.0 * above1 - above2, below2 - 8.0 * below1, below1)
                for spot, value in zip(spots, values):
                    ghost[pl.ds(first + spot, levels, stride=8)] = value
        for n in range(half):
            start = (parity * half + n) * levels
            partials = []
            for k in range(levels):
                at = start + k
                current = ghost[at * 8:at * 8 + 8] * drive[at] + still[at]
                if k > 0:
                    current = current + carry[at] * partials[-1]
                partials.append(current)
            solved = [partials[-1]]
            for k in range(levels - 2, -1, -1):
                solved.insert(0, partials[k] + ratio[start + k] * solved[0])
            for k in range(levels):
                rows[start + k] = solved[k]
            for k in range(0, levels, 2):
                both = jnp.where(low, pltpu.roll(solved[k], 6, 0), pltpu.roll(solved[k + 1], 2, 0))
                change[parity, (n * levels + k) * 4:(n * levels + k) * 4 + 8] = both
        cols[parity] = change[parity].T

    def drain(ref, sem):
        pltpu.make_async_copy(ref, ref, sem).wait()

    for parity in range(2):
        on, _ = edge_state(me, parity, total, across)
        for e in range(4):
            base = (parity * 4 + e) * across * half
            seam_hub = jnp.logical_and(on[e], am_hub == 1)

            @pl.when(seam_hub)
            def _():
                drain(s.at[parity, e, :, pl.ds(0, HUBS - 1)], send1.at[parity, e])
                drain(d.at[pl.ds(base, (across - 1) * half)], send2.at[parity, e])

            @pl.when(jnp.logical_not(seam_hub))
            def _():
                drain(s.at[parity, e], send1.at[parity, e])

            @pl.when(jnp.logical_and(jnp.logical_not(on[e]), am_hub == 1))
            def _():
                drain(d.at[pl.ds(base, across * half)], send2.at[parity, e])


def finish_kernel(u, cols, rows, result, out, out_sem):
    panels, levels, ct, _ = u.shape
    half = panels // 2
    size = 8
    wide = lax.broadcasted_iota(jnp.int32, (size, 128), 1)
    sub = lax.broadcasted_iota(jnp.int32, (size, 128), 0)
    edge = jnp.logical_or(wide < DEPTH, wide >= 128 - DEPTH)
    for p in range(panels):
        n, parity = p // 2, p % 2
        for k in range(levels):
            group = n * levels + k
            extra = rows[parity * half * levels + group]
            for start in range(0, ct, size):
                patch = pltpu.roll(cols[parity, start:start + size], (126 - 4 * group) % 128, 1)
                value = u[p, k, start:start + size] + jnp.where(edge, patch, 0.0)
                if start == 0:
                    value = value + jnp.where(sub < DEPTH, extra, 0.0)
                if start == ct - size:
                    value = value + jnp.where(sub >= size - DEPTH, extra, 0.0)
                out[p, k, start:start + size] = value
        pltpu.make_async_copy(out.at[p], result.at[p], out_sem.at[p]).start()
    for p in range(panels):
        pltpu.make_async_copy(out.at[p], result.at[p], out_sem.at[p]).wait()


def solution(mesh):
    total = mesh.shape["tile"]
    across = math.isqrt(total)

    def shards(tracer, courant_east, courant_north, diffusivity, seam_table):
        _, panels, levels, ct, _ = tracer.shape
        half, per = panels // 2, DEPTH * levels // HUBS
        strips = (2, 4, half, HUBS, per, ct)
        units = (2 * 4 * across * half, per, ct)
        packs = (panels * levels, 8, ct)
        shape = tracer.shape[1:]
        anywhere = pl.BlockSpec(memory_space=pl.ANY)
        hbm = pl.BlockSpec(memory_space=pltpu.HBM)
        whole = pl.BlockSpec(memory_space=pltpu.VMEM)
        table = jnp.transpose(seam_table, (2, 1, 0))
        plain, cols, rows = pl.pallas_call(
            functools.partial(exchange_kernel, total, across),
            out_shape=[pltpu.VMEM(dims, jnp.float32) for dims in (shape, (2, ct, ct), packs)],
            in_specs=[hbm] * 5,
            out_specs=[whole] * 3,
            scratch_shapes=[
                pltpu.SMEM(table.shape, jnp.int32),
                pltpu.VMEM(shape, jnp.float32),
                pltpu.VMEM(shape, jnp.bfloat16),
                pltpu.VMEM(shape, jnp.bfloat16),
                pltpu.VMEM(shape, jnp.bfloat16),
                pltpu.VMEM(strips, jnp.float32),
                pltpu.VMEM(units, jnp.float32),
                pltpu.VMEM(units, jnp.float32),
                pltpu.VMEM(strips, jnp.float32),
                pltpu.VMEM((2, ct, ct), jnp.float32),
                pltpu.VMEM(packs, jnp.float32),
                pltpu.VMEM(packs, jnp.float32),
                pltpu.VMEM(packs, jnp.float32),
                pltpu.VMEM(packs, jnp.float32),
                pltpu.VMEM((panels * levels * 8, ct), jnp.float32),
                pltpu.VMEM((2, ct, ct), jnp.float32),
                pltpu.SemaphoreType.DMA,
                pltpu.SemaphoreType.DMA((panels,)),
                pltpu.SemaphoreType.DMA((3, panels)),
                pltpu.SemaphoreType.DMA((2, 4)),
                pltpu.SemaphoreType.DMA,
                pltpu.SemaphoreType.DMA((2, 4)),
                pltpu.SemaphoreType.DMA((2, 4)),
                pltpu.SemaphoreType.REGULAR,
                pltpu.SemaphoreType.REGULAR,
            ],
            compiler_params=pltpu.CompilerParams(collective_id=0, has_side_effects=True,
                                                 vmem_limit_bytes=VMEM_LIMIT),
            name="exchange",
        )(table, tracer[0], courant_east[0], courant_north[0], diffusivity[0])
        updated = pl.pallas_call(
            finish_kernel,
            out_shape=jax.ShapeDtypeStruct(shape, jnp.float32),
            in_specs=[whole] * 3,
            out_specs=anywhere,
            scratch_shapes=[pltpu.VMEM(shape, jnp.float32), pltpu.SemaphoreType.DMA((panels,))],
            compiler_params=pltpu.CompilerParams(vmem_limit_bytes=VMEM_LIMIT // 2),
            name="finish",
        )(plain, cols, rows)
        return updated[None]

    placed = P(("groups", "tile"), None, None, None, None)
    return jax.shard_map(
        shards, mesh=mesh, in_specs=(placed, placed, placed, placed, P()), out_specs=placed,
        check_vma=False)
```

profile of v0, /device:TPU:0, one launch (start us, length us, event | category | flops | bytes accessed | tf_op | source)
XLA Modules:
  0.0 16.0 jit_solution(7310273698759701323)
XLA Ops:
  0.0 14.1 %exchange.1 = (f32[6,8,128,128]{3,2,1,0:T(8,128)S(1)}, f32[2,128,128]{2,1,0:T(8,128)S(1)}, f32[48,8,128]{2,1,0:T(8,128)S(1)}) custom-call(s32[3,4,6]{2,1,0:T(4,128)} %bitcast.10, f32[6,8,128,128]{3,2,1,0:T(8,128)} %bitcast.6, bf16[6,8,128,128]{3,2,1,0:T(8,128)(2,1)} %bitcast.7, bf16[6,8,128,128]{3,2,1,0:T(8,128)(2,1)} %bitcast.8, ...), custom_call_target="tpu_custom_call" | custom-call | tf_op jit(solution)/shard_map/exchange/pallas_call | solution.py:442
  14.1 1.9 %finish.1 = f32[6,8,128,128]{3,2,1,0:T(8,128)} custom-call(f32[6,8,128,128]{3,2,1,0:T(8,128)S(1)} %get-tuple-element.8.u, f32[2,128,128]{2,1,0:T(8,128)S(1)} %get-tuple-element.9.cols, f32[48,8,128]{2,1,0:T(8,128)S(1)} %get-tuple-element.10.rows), custom_call_target="tpu_custom_call" | custom-call | tf_op jit(solution)/shard_map/finish/pallas_call | solution.py:478
where the time goes:
time: 16.2 us; the launch traced here: 16 us
  Pallas kernels  16 us (99%)
    pallas_call x1, Pallas kernels, shards(): pl.pallas_call(functools.partial(exchange_kernel, total, across), out_sha...  14.1 us
    pallas_call x1, Pallas kernels, shards(): pl.pallas_call(finish_kernel, out_shape=jax.ShapeDtypeStruct(shape, jnp.f...  1.91 us

commit v1 on v0

--- a/solution.py
+++ b/solution.py
@@ -10,6 +10,7 @@
 
 DEPTH = 2
 HUBS = 4
+LEVELS_AT_ONCE = 2
 VMEM_LIMIT = 59 * 1024 * 1024
 
 
@@ -22,6 +23,11 @@
     row, col = tile // across, lax.rem(tile, across)
     on = (col == 0, row == across - 1, col == across - 1, row == 0)
     return on, (row, col, row, col)
+
+
+def hubs_of(total, across):
+    middle = total // 2
+    return (middle - across + 1, middle - across + 3, middle + 1, middle + 3)
 
 
 def edge_tile(edge, spot, across):
@@ -125,20 +131,27 @@
 
 
 def exchange_kernel(total, across, table_in, tracer, east_in, north_in, coupling_in, u, cols, rows,
-                    table, q, east, north, coupling, s, r, d, h, own, drive, carry, ratio, still, ghost, change,
+                    table, route, q, east, north, coupling, s, r, d, h, own, drive, carry, ratio, still, ghost, change,
                     t_sem, q_sem, c_sem, send1, r_sem, send2, h_sem, peer, ready):
     panels, levels, ct, _ = q.shape
     half = panels // 2
     per = DEPTH * levels // HUBS
-    first_hub = total // 2 - HUBS + 1
+    hubs = hubs_of(total, across)
     me = lax.axis_index("tile")
     steps = (total - 1, across, 1, total - across)
     offsets = sorted(set(steps))
 
     def hub_flag(device):
-        ahead = device - first_hub
-        inside = jnp.logical_and(ahead >= 0, ahead < 2 * HUBS)
-        return jnp.where(jnp.logical_and(inside, lax.rem(ahead + total, 2) == 0), 1, 0)
+        flag = jnp.where(device == hubs[0], 1, 0)
+        for hub in hubs[1:]:
+            flag = flag + jnp.where(device == hub, 1, 0)
+        return flag
+
+    def hub_at(i):
+        hub = hubs[0]
+        for j in range(1, HUBS):
+            hub = jnp.where(i == j, hubs[j], hub)
+        return hub
 
     am_hub = hub_flag(me)
 
@@ -192,36 +205,53 @@
 
     flat = q.reshape(panels * levels * ct, 128)
     blocks = levels // per
-    for parity in range(2):
-        gathered = jnp.zeros((ct, 128), jnp.float32)
-        for n in range(half):
-            p = 2 * n + parity
-            load(p).wait()
-            gathered = gather_columns(q, p, n, gathered)
-            for block in range(blocks):
-                for depth in range(DEPTH):
-                    x, base = depth * blocks + block, (p * levels + block * per) * ct
-                    s[parity, 3, n, x] = flat[pl.ds(base + depth, per, stride=ct)]
-                    s[parity, 1, n, x] = flat[pl.ds(base + ct - 1 - depth, per, stride=ct)]
+    early = me < across
+    late = jnp.logical_not(early)
+    deferred = jnp.logical_or(early, am_hub == 1)
+
+    def prepare_rows(parity, n):
+        p = 2 * n + parity
+        for block in range(blocks):
+            for depth in range(DEPTH):
+                x, base = depth * blocks + block, (p * levels + block * per) * ct
+                s[parity, 3, n, x] = flat[pl.ds(base + depth, per, stride=ct)]
+                s[parity, 1, n, x] = flat[pl.ds(base + ct - 1 - depth, per, stride=ct)]
+
+    def finish_columns(parity, gathered):
         own[parity] = gathered.T
         for n in range(half):
             for block in range(blocks):
                 base = (n * levels + block * per) * 4
                 for c, (e, depth) in enumerate(((2, 1), (2, 0), (0, 0), (0, 1))):
                     s[parity, e, n, depth * blocks + block] = own[parity, pl.ds(base + c, per, stride=4)]
-        if parity == 0:
-            for n in range(half):
-                for copy in loads(n):
-                    copy.start()
-            pl.semaphore_wait(barrier, expected)
+
+    def enter():
+        pl.semaphore_wait(barrier, expected)
+
+        @pl.when(am_hub == 0)
+        def _():
+            for offset in offsets:
+                other = lax.rem(me + offset, total)
+
+                @pl.when(other < me)
+                def _():
+                    signal(peer, other)
+
+        for hub in hubs:
+            @pl.when(me != hub)
+            def _():
+                signal(ready, hub)
+
+    def send_seams(parity, edges):
         on, along = edge_state(me, parity, total, across)
-        for e in range(4):
+        for e in edges:
             @pl.when(on[e])
             def _():
                 slot = ((parity * 4 + e) * across + along[e]) * half
 
-                def spread(i, carry):
-                    hub = first_hub + 2 * i
+                def spread(step, carry):
+                    i = jnp.where(me * 2 < total, HUBS - 1 - step, step)
+                    hub = hub_at(i)
                     src, dst = s.at[parity, e, :, i], r.at[pl.ds(slot, half)]
 
                     @pl.when(hub != me)
@@ -236,76 +266,113 @@
 
                 lax.fori_loop(0, HUBS, spread, 0)
 
-    for n in range(half, panels):
-        for copy in loads(n):
-            copy.start()
-
-    @pl.when(am_hub == 0)
-    def _():
-        for offset in offsets:
-            other = lax.rem(me + offset, total)
-
-            @pl.when(other < me)
-            def _():
-                signal(peer, other)
-
-    for i in range(HUBS):
-        @pl.when(me != first_hub + 2 * i)
+    def send_neighbours():
+        @pl.when(peers > 0)
         def _():
-            signal(ready, first_hub + 2 * i)
-
-    @pl.when(peers > 0)
-    def _():
-        pl.semaphore_wait(peer, peers)
-
-    for parity in range(2):
-        on, _ = edge_state(me, parity, total, across)
-        for e in range(4):
-            @pl.when(jnp.logical_not(on[e]))
-            def _():
-                far = (e + 2) % 4
-                remote(s.at[parity, e], h.at[parity, far], send1.at[parity, e],
-                       h_sem.at[parity, far], lax.rem(me + steps[e], total)).start()
+            pl.semaphore_wait(peer, peers)
+
+        for parity in range(2):
+            on, _ = edge_state(me, parity, total, across)
+            for e in range(4):
+                @pl.when(jnp.logical_not(on[e]))
+                def _():
+                    far = (e + 2) % 4
+                    remote(s.at[parity, e], h.at[parity, far], send1.at[parity, e],
+                           h_sem.at[parity, far], lax.rem(me + steps[e], total)).start()
+
+    for parity in range(2):
+        gathered = jnp.zeros((ct, 128), jnp.float32)
+        for n in range(half):
+            load(2 * n + parity).wait()
+            prepare_rows(parity, n)
+            if n == 0 and parity == 0:
+                gathered = gather_columns(q, parity, n, gathered)
+        for n in (range(half) if parity == 0 else range(half, panels)):
+            for copy in loads(n):
+                copy.start()
+
+        @pl.when(late)
+        def _():
+            if parity == 0:
+                enter()
+            send_seams(parity, (1, 3))
+
+        for n in range(1 - parity, half):
+            gathered = gather_columns(q, 2 * n + parity, n, gathered)
+        finish_columns(parity, gathered)
+
+        @pl.when(late)
+        def _():
+            send_seams(parity, (0, 2))
+
+    @pl.when(early)
+    def _():
+        enter()
+        for parity in range(2):
+            send_seams(parity, range(4))
+
+    @pl.when(jnp.logical_not(deferred))
+    def _():
+        send_neighbours()
+
+    def arrive(which):
+        for p in which:
+            for copy in loads(p):
+                copy.wait()
 
     def compute(first, last):
         def one(p, carry):
-            for copy in loads(p):
-                copy.wait()
             update_panel(q, east, north, coupling, u, p)
             return carry
 
         lax.fori_loop(first, last, one, 0)
 
+    fetch.wait()
+    seams = [(edge_tile(e, spot, across) + parity * (total // 2 + 1), parity, e, spot)
+             for parity in range(2) for e in range(4) for spot in range(across)]
+    seams = sorted((tile % total, *rest) for tile, *rest in seams)
+
+    @pl.when(am_hub == 1)
+    def _():
+        for e in range(4):
+            for p in range(panels):
+                other, f, turn = table[0, e, p], table[1, e, p], table[2, e, p]
+                base = (lax.rem(other, 2) * 4 + f) * across * half + other // 2
+                base = jnp.where(turn == 1, base + (across - 1) * half, base)
+                step = jnp.where(turn == 1, -half, half)
+                for spot in range(across):
+                    route[((p % 2 * 4 + e) * across + spot) * half + p // 2] = base + step * spot
+
+    arrive(range(half))
     compute(0, half)
-    fetch.wait()
+
+    @pl.when(deferred)
+    def _():
+        send_neighbours()
 
     @pl.when(am_hub == 1)
     def _():
         pl.semaphore_wait(ready, total - 1)
         pltpu.make_async_copy(r, r, r_sem).wait()
-        seams = [(edge_tile(e, spot, across) + parity * (total // 2 + 1), parity, e, spot)
-                 for parity in range(2) for e in range(4) for spot in range(across)]
-        for owner, parity, e, spot in sorted((tile % total, *rest) for tile, *rest in seams):
+        place = jnp.where(me == hubs[1], 1, 0) + jnp.where(me == hubs[2], 2, 0) + jnp.where(me == hubs[3], 3, 0)
+        for owner, parity, e, spot in seams:
             slot = ((parity * 4 + e) * across + spot) * half
             for n in range(half):
-                p = 2 * n + parity
-                other, f, turn = table[0, e, p], table[1, e, p], table[2, e, p]
-                base = (lax.rem(other, 2) * 4 + f) * across * half + other // 2
-                place = jnp.where(turn == 1, across - 1 - spot, spot)
-                d[slot + n] = r[base + place * half]
+                d[slot + n] = r[route[slot + n]]
             src = d.at[pl.ds(slot, half)]
-            dst = h.at[parity, e, :, (me - first_hub) // 2]
-
-            @pl.when(me != owner)
-            def _():
+            dst = h.at[parity, e, :, place]
+            if owner in hubs:
+                @pl.when(me != owner)
+                def _():
+                    remote(src, dst, send2.at[parity, e], h_sem.at[parity, e], owner).start()
+
+                @pl.when(me == owner)
+                def _():
+                    pltpu.make_async_copy(src, dst, h_sem.at[parity, e]).start()
+            else:
                 remote(src, dst, send2.at[parity, e], h_sem.at[parity, e], owner).start()
 
-            @pl.when(me == owner)
-            def _():
-                pltpu.make_async_copy(src, dst, h_sem.at[parity, e]).start()
-
-    compute(half, panels)
-
+    arrive(range(half, panels))
     sub = lax.broadcasted_iota(jnp.int32, (8, 128), 0)
     low, inner = sub < 4, jnp.logical_and(sub >= 2, sub < 6)
     for parity in range(2):
@@ -333,12 +400,37 @@
                     carry[spot] = inverses[k] * below
                 below = jnp.where(inner, packed_columns(coupling_columns, group), packed_rows(coupling, p, k, low))
 
+    compute(half, panels)
+
+    def drain(ref, sem):
+        pltpu.make_async_copy(ref, ref, sem).wait()
+
+    for parity in range(2):
+        on, _ = edge_state(me, parity, total, across)
+        for e in range(4):
+            base = (parity * 4 + e) * across * half
+            seam_hub = jnp.logical_and(on[e], am_hub == 1)
+
+            @pl.when(seam_hub)
+            def _():
+                drain(s.at[parity, e, :, pl.ds(0, HUBS - 1)], send1.at[parity, e])
+                drain(d.at[pl.ds(base, (across - 1) * half)], send2.at[parity, e])
+
+            @pl.when(jnp.logical_not(seam_hub))
+            def _():
+                drain(s.at[parity, e], send1.at[parity, e])
+
+            @pl.when(jnp.logical_and(jnp.logical_not(on[e]), am_hub == 1))
+            def _():
+                drain(d.at[pl.ds(base, across * half)], send2.at[parity, e])
+
     lane = lax.broadcasted_iota(jnp.int32, (levels, 128), 1)
     change[...] = jnp.zeros_like(change)
     for parity in range(2):
+        for e in range(4):
+            drain(h.at[parity, e], h_sem.at[parity, e])
+    for parity in range(2):
         on, _ = edge_state(me, parity, total, across)
-        for e in range(4):
-            pltpu.make_async_copy(h.at[parity, e], h.at[parity, e], h_sem.at[parity, e]).wait()
         for n in range(half):
             p = 2 * n + parity
             first = (parity * half + n) * levels * 8
@@ -357,6 +449,7 @@
                 values = (-above1, 8.0 * above1 - above2, below2 - 8.0 * below1, below1)
                 for spot, value in zip(spots, values):
                     ghost[pl.ds(first + spot, levels, stride=8)] = value
+    for parity in range(2):
         for n in range(half):
             start = (parity * half + n) * levels
             partials = []
@@ -374,29 +467,8 @@
             for k in range(0, levels, 2):
                 both = jnp.where(low, pltpu.roll(solved[k], 6, 0), pltpu.roll(solved[k + 1], 2, 0))
                 change[parity, (n * levels + k) * 4:(n * levels + k) * 4 + 8] = both
+    for parity in range(2):
         cols[parity] = change[parity].T
-
-    def drain(ref, sem):
-        pltpu.make_async_copy(ref, ref, sem).wait()
-
-    for parity in range(2):
-        on, _ = edge_state(me, parity, total, across)
-        for e in range(4):
-            base = (parity * 4 + e) * across * half
-            seam_hub = jnp.logical_and(on[e], am_hub == 1)
-
-            @pl.when(seam_hub)
-            def _():
-                drain(s.at[parity, e, :, pl.ds(0, HUBS - 1)], send1.at[parity, e])
-                drain(d.at[pl.ds(base, (across - 1) * half)], send2.at[parity, e])
-
-            @pl.when(jnp.logical_not(seam_hub))
-            def _():
-                drain(s.at[parity, e], send1.at[parity, e])
-
-            @pl.when(jnp.logical_and(jnp.logical_not(on[e]), am_hub == 1))
-            def _():
-                drain(d.at[pl.ds(base, across * half)], send2.at[parity, e])
 
 
 def finish_kernel(u, cols, rows, result, out, out_sem):
@@ -406,6 +478,11 @@
     wide = lax.broadcasted_iota(jnp.int32, (size, 128), 1)
     sub = lax.broadcasted_iota(jnp.int32, (size, 128), 0)
     edge = jnp.logical_or(wide < DEPTH, wide >= 128 - DEPTH)
+
+    def store(p, block):
+        part = pl.ds(block * LEVELS_AT_ONCE, LEVELS_AT_ONCE)
+        return pltpu.make_async_copy(out.at[p, part], result.at[p, part], out_sem.at[p, block])
+
     for p in range(panels):
         n, parity = p // 2, p % 2
         for k in range(levels):
@@ -419,9 +496,11 @@
                 if start == ct - size:
                     value = value + jnp.where(sub >= size - DEPTH, extra, 0.0)
                 out[p, k, start:start + size] = value
-        pltpu.make_async_copy(out.at[p], result.at[p], out_sem.at[p]).start()
+            if k % LEVELS_AT_ONCE == LEVELS_AT_ONCE - 1:
+                store(p, k // LEVELS_AT_ONCE).start()
     for p in range(panels):
-        pltpu.make_async_copy(out.at[p], result.at[p], out_sem.at[p]).wait()
+        for block in range(levels // LEVELS_AT_ONCE):
+            store(p, block).wait()
 
 
 def solution(mesh):
@@ -446,6 +525,7 @@
             out_specs=[whole] * 3,
             scratch_shapes=[
                 pltpu.SMEM(table.shape, jnp.int32),
+                pltpu.SMEM(units[:1], jnp.int32),
                 pltpu.VMEM(shape, jnp.float32),
                 pltpu.VMEM(shape, jnp.bfloat16),
                 pltpu.VMEM(shape, jnp.bfloat16),
@@ -480,7 +560,7 @@
             out_shape=jax.ShapeDtypeStruct(shape, jnp.float32),
             in_specs=[whole] * 3,
             out_specs=anywhere,
-            scratch_shapes=[pltpu.VMEM(shape, jnp.float32), pltpu.SemaphoreType.DMA((panels,))],
+            scratch_shapes=[pltpu.VMEM(shape, jnp.float32), pltpu.SemaphoreType.DMA((panels, levels // LEVELS_AT_ONCE))],
             compiler_params=pltpu.CompilerParams(vmem_limit_bytes=VMEM_LIMIT // 2),
             name="finish",
         )(plain, cols, rows)

time: 16.2 us -> 15.2 us (0.938)
  Pallas kernels: 16 us -> 15.1 us
    pallas_call x1, Pallas kernels: 14.1 us -> 13.1 us  [shards(): pl.pallas_call(functools.partial(exchange_kernel, total, across), out_sha...]
where the time goes in v1:
time: 15.2 us; the launch traced here: 15.1 us
  Pallas kernels  15.1 us (99%)
    pallas_call x1, Pallas kernels, shards(): pl.pallas_call(functools.partial(exchange_kernel, total, across), out_sha...  13.1 us
    pallas_call x1, Pallas kernels, shards(): pl.pallas_call(finish_kernel, out_shape=jax.ShapeDtypeStruct(shape, jnp.f...  1.95 us

profile of v1, /device:TPU:0, one launch (start us, length us, event | category | flops | bytes accessed | tf_op | source)
XLA Modules:
  0.0 15.1 jit_solution(14208860952434116853)
XLA Ops:
  0.0 13.1 %exchange.1 = (f32[6,8,128,128]{3,2,1,0:T(8,128)S(1)}, f32[2,128,128]{2,1,0:T(8,128)S(1)}, f32[48,8,128]{2,1,0:T(8,128)S(1)}) custom-call(s32[3,4,6]{2,1,0:T(4,128)} %bitcast.10, f32[6,8,128,128]{3,2,1,0:T(8,128)} %bitcast.6, bf16[6,8,128,128]{3,2,1,0:T(8,128)(2,1)} %bitcast.7, bf16[6,8,128,128]{3,2,1,0:T(8,128)(2,1)} %bitcast.8, ...), custom_call_target="tpu_custom_call" | custom-call | tf_op jit(solution)/shard_map/exchange/pallas_call | solution.py:521
  13.1 2.0 %finish.1 = f32[6,8,128,128]{3,2,1,0:T(8,128)} custom-call(f32[6,8,128,128]{3,2,1,0:T(8,128)S(1)} %get-tuple-element.8.u, f32[2,128,128]{2,1,0:T(8,128)S(1)} %get-tuple-element.9.cols, f32[48,8,128]{2,1,0:T(8,128)S(1)} %get-tuple-element.10.rows), custom_call_target="tpu_custom_call" | custom-call | tf_op jit(solution)/shard_map/finish/pallas_call | solution.py:558

commit v2 on v1

--- a/solution.py
+++ b/solution.py
@@ -27,7 +27,7 @@
 
 def hubs_of(total, across):
     middle = total // 2
-    return (middle - across + 1, middle - across + 3, middle + 1, middle + 3)
+    return (middle - across, middle - across + 1, middle - across + 3, middle + 1)
 
 
 def edge_tile(edge, spot, across):
@@ -131,7 +131,7 @@
 
 
 def exchange_kernel(total, across, table_in, tracer, east_in, north_in, coupling_in, u, cols, rows,
-                    table, route, q, east, north, coupling, s, r, d, h, own, drive, carry, ratio, still, ghost, change,
+                    table, route, q, fields, s, r, d, h, own, drive, carry, ratio, still, ghost, change,
                     t_sem, q_sem, c_sem, send1, r_sem, send2, h_sem, peer, ready):
     panels, levels, ct, _ = q.shape
     half = panels // 2
@@ -147,25 +147,28 @@
             flag = flag + jnp.where(device == hub, 1, 0)
         return flag
 
-    def hub_at(i):
-        hub = hubs[0]
-        for j in range(1, HUBS):
-            hub = jnp.where(i == j, hubs[j], hub)
-        return hub
-
     am_hub = hub_flag(me)
 
-    def load(p):
-        return pltpu.make_async_copy(tracer.at[p], q.at[p], q_sem.at[p])
-
-    fields = ((east_in, east), (north_in, north), (coupling_in, coupling))
-
-    def loads(p):
-        return [pltpu.make_async_copy(src.at[p], dst.at[p], c_sem.at[i, p]) for i, (src, dst) in enumerate(fields)]
-
-    for parity in range(2):
-        for n in range(half):
-            load(2 * n + parity).start()
+    def load(p, stage):
+        pltpu.make_async_copy(tracer.at[p], q.at[p], q_sem.at[stage]).start()
+
+    def drain(ref, sem):
+        pltpu.make_async_copy(ref, ref, sem).wait()
+
+    def load_fields(stage):
+        part = pl.ds(stage * half, half)
+        for i, src in enumerate((east_in, north_in, coupling_in)):
+            pltpu.make_async_copy(src.at[part], fields.at[i, part], c_sem.at[stage]).start()
+
+    def arrive(stage):
+        drain(fields.at[:, pl.ds(stage * half, half)], c_sem.at[stage])
+
+    east, north, coupling = (fields.at[i] for i in range(3))
+    load(0, 0)
+    for n in range(1, half):
+        load(2 * n, 1)
+    for n in range(half):
+        load(2 * n + 1, 2)
     fetch = pltpu.make_async_copy(table_in, table, t_sem)
     fetch.start()
 
@@ -225,9 +228,7 @@
                 for c, (e, depth) in enumerate(((2, 1), (2, 0), (0, 0), (0, 1))):
                     s[parity, e, n, depth * blocks + block] = own[parity, pl.ds(base + c, per, stride=4)]
 
-    def enter():
-        pl.semaphore_wait(barrier, expected)
-
+    def tell():
         @pl.when(am_hub == 0)
         def _():
             for offset in offsets:
@@ -242,29 +243,34 @@
             def _():
                 signal(ready, hub)
 
-    def send_seams(parity, edges):
+    def send_seams(parity, edges, order):
         on, along = edge_state(me, parity, total, across)
         for e in edges:
             @pl.when(on[e])
             def _():
                 slot = ((parity * 4 + e) * across + along[e]) * half
 
-                def spread(step, carry):
-                    i = jnp.where(me * 2 < total, HUBS - 1 - step, step)
-                    hub = hub_at(i)
-                    src, dst = s.at[parity, e, :, i], r.at[pl.ds(slot, half)]
-
-                    @pl.when(hub != me)
-                    def _():
-                        remote(src, dst, send1.at[parity, e], r_sem, hub).start()
-
-                    @pl.when(hub == me)
-                    def _():
-                        pltpu.make_async_copy(src, dst, r_sem).start()
-
-                    return carry
-
-                lax.fori_loop(0, HUBS, spread, 0)
+                def piece(i):
+                    return s.at[parity, e, :, i], r.at[pl.ds(slot, half)]
+
+                @pl.when(am_hub == 0)
+                def _():
+                    for i in order:
+                        src, dst = piece(i)
+                        remote(src, dst, send1, r_sem, hubs[i]).start()
+
+                @pl.when(am_hub == 1)
+                def _():
+                    for i in order:
+                        src, dst = piece(i)
+
+                        @pl.when(me != hubs[i])
+                        def _():
+                            remote(src, dst, send1, r_sem, hubs[i]).start()
+
+                        @pl.when(me == hubs[i])
+                        def _():
+                            pltpu.make_async_copy(src, dst, r_sem).start()
 
     def send_neighbours():
         @pl.when(peers > 0)
@@ -277,25 +283,29 @@
                 @pl.when(jnp.logical_not(on[e]))
                 def _():
                     far = (e + 2) % 4
-                    remote(s.at[parity, e], h.at[parity, far], send1.at[parity, e],
-                           h_sem.at[parity, far], lax.rem(me + steps[e], total)).start()
+                    remote(s.at[parity, e], h.at[parity, far], send1, h_sem,
+                           lax.rem(me + steps[e], total)).start()
 
     for parity in range(2):
         gathered = jnp.zeros((ct, 128), jnp.float32)
-        for n in range(half):
-            load(2 * n + parity).wait()
+        if parity == 0:
+            drain(q.at[0], q_sem.at[0])
+            prepare_rows(0, 0)
+            gathered = gather_columns(q, 0, 0, gathered)
+            drain(q.at[pl.ds(0, half - 1)], q_sem.at[1])
+        else:
+            drain(q.at[pl.ds(0, half)], q_sem.at[2])
+        for n in range(1 - parity, half):
             prepare_rows(parity, n)
-            if n == 0 and parity == 0:
-                gathered = gather_columns(q, parity, n, gathered)
-        for n in (range(half) if parity == 0 else range(half, panels)):
-            for copy in loads(n):
-                copy.start()
+        load_fields(parity)
 
         @pl.when(late)
         def _():
             if parity == 0:
-                enter()
-            send_seams(parity, (1, 3))
+                pl.semaphore_wait(barrier, expected)
+            send_seams(parity, (1, 3), range(HUBS))
+            if parity == 0:
+                tell()
 
         for n in range(1 - parity, half):
             gathered = gather_columns(q, 2 * n + parity, n, gathered)
@@ -303,22 +313,18 @@
 
         @pl.when(late)
         def _():
-            send_seams(parity, (0, 2))
+            send_seams(parity, (0, 2), range(HUBS))
 
     @pl.when(early)
     def _():
-        enter()
+        pl.semaphore_wait(barrier, expected)
         for parity in range(2):
-            send_seams(parity, range(4))
+            send_seams(parity, range(4), range(HUBS - 1, -1, -1))
+        tell()
 
     @pl.when(jnp.logical_not(deferred))
     def _():
         send_neighbours()
-
-    def arrive(which):
-        for p in which:
-            for copy in loads(p):
-                copy.wait()
 
     def compute(first, last):
         def one(p, carry):
@@ -343,7 +349,7 @@
                 for spot in range(across):
                     route[((p % 2 * 4 + e) * across + spot) * half + p // 2] = base + step * spot
 
-    arrive(range(half))
+    arrive(0)
     compute(0, half)
 
     @pl.when(deferred)
@@ -364,15 +370,15 @@
             if owner in hubs:
                 @pl.when(me != owner)
                 def _():
-                    remote(src, dst, send2.at[parity, e], h_sem.at[parity, e], owner).start()
+                    remote(src, dst, send2, h_sem, owner).start()
 
                 @pl.when(me == owner)
                 def _():
-                    pltpu.make_async_copy(src, dst, h_sem.at[parity, e]).start()
+                    pltpu.make_async_copy(src, dst, h_sem).start()
             else:
-                remote(src, dst, send2.at[parity, e], h_sem.at[parity, e], owner).start()
-
-    arrive(range(half, panels))
+                remote(src, dst, send2, h_sem, owner).start()
+
+    arrive(1)
     sub = lax.broadcasted_iota(jnp.int32, (8, 128), 0)
     low, inner = sub < 4, jnp.logical_and(sub >= 2, sub < 6)
     for parity in range(2):
@@ -402,33 +408,23 @@
 
     compute(half, panels)
 
-    def drain(ref, sem):
-        pltpu.make_async_copy(ref, ref, sem).wait()
-
+    seam_edges = 0
     for parity in range(2):
         on, _ = edge_state(me, parity, total, across)
         for e in range(4):
-            base = (parity * 4 + e) * across * half
-            seam_hub = jnp.logical_and(on[e], am_hub == 1)
-
-            @pl.when(seam_hub)
-            def _():
-                drain(s.at[parity, e, :, pl.ds(0, HUBS - 1)], send1.at[parity, e])
-                drain(d.at[pl.ds(base, (across - 1) * half)], send2.at[parity, e])
-
-            @pl.when(jnp.logical_not(seam_hub))
-            def _():
-                drain(s.at[parity, e], send1.at[parity, e])
-
-            @pl.when(jnp.logical_and(jnp.logical_not(on[e]), am_hub == 1))
-            def _():
-                drain(d.at[pl.ds(base, across * half)], send2.at[parity, e])
+            seam_edges = seam_edges + jnp.where(on[e], 1, 0)
+    for count in range(5):
+        @pl.when(seam_edges * am_hub == count)
+        def _():
+            drain(r.at[pl.ds(0, (8 * HUBS - count) * half)], send1)
+
+        @pl.when(jnp.logical_and(seam_edges == count, am_hub == 1))
+        def _():
+            drain(d.at[pl.ds(0, (8 * across - count) * half)], send2)
 
     lane = lax.broadcasted_iota(jnp.int32, (levels, 128), 1)
     change[...] = jnp.zeros_like(change)
-    for parity in range(2):
-        for e in range(4):
-            drain(h.at[parity, e], h_sem.at[parity, e])
+    drain(h, h_sem)
     for parity in range(2):
         on, _ = edge_state(me, parity, total, across)
         for n in range(half):
@@ -481,7 +477,7 @@
 
     def store(p, block):
         part = pl.ds(block * LEVELS_AT_ONCE, LEVELS_AT_ONCE)
-        return pltpu.make_async_copy(out.at[p, part], result.at[p, part], out_sem.at[p, block])
+        return pltpu.make_async_copy(out.at[p, part], result.at[p, part], out_sem)
 
     for p in range(panels):
         n, parity = p // 2, p % 2
@@ -498,9 +494,7 @@
                 out[p, k, start:start + size] = value
             if k % LEVELS_AT_ONCE == LEVELS_AT_ONCE - 1:
                 store(p, k // LEVELS_AT_ONCE).start()
-    for p in range(panels):
-        for block in range(levels // LEVELS_AT_ONCE):
-            store(p, block).wait()
+    pltpu.make_async_copy(out, result, out_sem).wait()
 
 
 def solution(mesh):
@@ -527,9 +521,7 @@
                 pltpu.SMEM(table.shape, jnp.int32),
                 pltpu.SMEM(units[:1], jnp.int32),
                 pltpu.VMEM(shape, jnp.float32),
-                pltpu.VMEM(shape, jnp.bfloat16),
-                pltpu.VMEM(shape, jnp.bfloat16),
-                pltpu.VMEM(shape, jnp.bfloat16),
+                pltpu.VMEM((3,) + shape, jnp.bfloat16),
                 pltpu.VMEM(strips, jnp.float32),
                 pltpu.VMEM(units, jnp.float32),
                 pltpu.VMEM(units, jnp.float32),
@@ -542,12 +534,12 @@
                 pltpu.VMEM((panels * levels * 8, ct), jnp.float32),
                 pltpu.VMEM((2, ct, ct), jnp.float32),
                 pltpu.SemaphoreType.DMA,
-                pltpu.SemaphoreType.DMA((panels,)),
-                pltpu.SemaphoreType.DMA((3, panels)),
-                pltpu.SemaphoreType.DMA((2, 4)),
+                pltpu.SemaphoreType.DMA((3,)),
+                pltpu.SemaphoreType.DMA((2,)),
                 pltpu.SemaphoreType.DMA,
-                pltpu.SemaphoreType.DMA((2, 4)),
-                pltpu.SemaphoreType.DMA((2, 4)),
+                pltpu.SemaphoreType.DMA,
+                pltpu.SemaphoreType.DMA,
+                pltpu.SemaphoreType.DMA,
                 pltpu.SemaphoreType.REGULAR,
                 pltpu.SemaphoreType.REGULAR,
             ],
@@ -560,7 +552,7 @@
             out_shape=jax.ShapeDtypeStruct(shape, jnp.float32),
             in_specs=[whole] * 3,
             out_specs=anywhere,
-            scratch_shapes=[pltpu.VMEM(shape, jnp.float32), pltpu.SemaphoreType.DMA((panels, levels // LEVELS_AT_ONCE))],
+            scratch_shapes=[pltpu.VMEM(shape, jnp.float32), pltpu.SemaphoreType.DMA],
             compiler_params=pltpu.CompilerParams(vmem_limit_bytes=VMEM_LIMIT // 2),
             name="finish",
         )(plain, cols, rows)

time: 15.2 us -> 14.2 us (0.934)
  Pallas kernels: 15.1 us -> 14.1 us
    pallas_call x1, Pallas kernels: 13.1 us -> 12.3 us  [shards(): pl.pallas_call(functools.partial(exchange_kernel, total, across), out_sha...]
    pallas_call x1, Pallas kernels: 1.95 us -> 1.75 us  [shards(): pl.pallas_call(finish_kernel, out_shape=jax.ShapeDtypeStruct(shape, jnp.f...]
where the time goes in v2:
time: 14.2 us; the launch traced here: 14.1 us
  Pallas kernels  14.1 us (99%)
    pallas_call x1, Pallas kernels, shards(): pl.pallas_call(functools.partial(exchange_kernel, total, across), out_sha...  12.3 us
    pallas_call x1, Pallas kernels, shards(): pl.pallas_call(finish_kernel, out_shape=jax.ShapeDtypeStruct(shape, jnp.f...  1.75 us

profile of v2, /device:TPU:0, one launch (start us, length us, event | category | flops | bytes accessed | tf_op | source)
XLA Modules:
  0.0 14.1 jit_solution(16044545051358675200)
XLA Ops:
  0.0 12.3 %exchange.1 = (f32[6,8,128,128]{3,2,1,0:T(8,128)S(1)}, f32[2,128,128]{2,1,0:T(8,128)S(1)}, f32[48,8,128]{2,1,0:T(8,128)S(1)}) custom-call(s32[3,4,6]{2,1,0:T(4,128)} %bitcast.10, f32[6,8,128,128]{3,2,1,0:T(8,128)} %bitcast.6, bf16[6,8,128,128]{3,2,1,0:T(8,128)(2,1)} %bitcast.7, bf16[6,8,128,128]{3,2,1,0:T(8,128)(2,1)} %bitcast.8, ...), custom_call_target="tpu_custom_call" | custom-call | tf_op jit(solution)/shard_map/exchange/pallas_call | solution.py:515
  12.4 1.7 %finish.1 = f32[6,8,128,128]{3,2,1,0:T(8,128)} custom-call(f32[6,8,128,128]{3,2,1,0:T(8,128)S(1)} %get-tuple-element.8.u, f32[2,128,128]{2,1,0:T(8,128)S(1)} %get-tuple-element.9.cols, f32[48,8,128]{2,1,0:T(8,128)S(1)} %get-tuple-element.10.rows), custom_call_target="tpu_custom_call" | custom-call | tf_op jit(solution)/shard_map/finish/pallas_call | solution.py:550

commit v3 on v2

--- a/solution.py
+++ b/solution.py
@@ -27,7 +27,7 @@
 
 def hubs_of(total, across):
     middle = total // 2
-    return (middle - across, middle - across + 1, middle - across + 3, middle + 1)
+    return (middle - across - 1, middle - across + 1, middle - across + 3, middle + 1)
 
 
 def edge_tile(edge, spot, across):
@@ -304,8 +304,6 @@
             if parity == 0:
                 pl.semaphore_wait(barrier, expected)
             send_seams(parity, (1, 3), range(HUBS))
-            if parity == 0:
-                tell()
 
         for n in range(1 - parity, half):
             gathered = gather_columns(q, 2 * n + parity, n, gathered)
@@ -314,6 +312,8 @@
         @pl.when(late)
         def _():
             send_seams(parity, (0, 2), range(HUBS))
+            if parity == 1:
+                tell()
 
     @pl.when(early)
     def _():

time: 14.2 us -> 14 us (0.986)
  Pallas kernels: 14.1 us -> 13.9 us
    pallas_call x1, Pallas kernels: 12.3 us -> 12.1 us  [shards(): pl.pallas_call(functools.partial(exchange_kernel, total, across), out_sha...]
where the time goes in v3:
time: 14 us; the launch traced here: 13.9 us
  Pallas kernels  13.9 us (99%)
    pallas_call x1, Pallas kernels, shards(): pl.pallas_call(functools.partial(exchange_kernel, total, across), out_sha...  12.1 us
    pallas_call x1, Pallas kernels, shards(): pl.pallas_call(finish_kernel, out_shape=jax.ShapeDtypeStruct(shape, jnp.f...  1.75 us

profile of v3, /device:TPU:0, one launch (start us, length us, event | category | flops | bytes accessed | tf_op | source)
XLA Modules:
  0.0 13.9 jit_solution(10930042699629377786)
XLA Ops:
  0.0 12.1 %exchange.1 = (f32[6,8,128,128]{3,2,1,0:T(8,128)S(1)}, f32[2,128,128]{2,1,0:T(8,128)S(1)}, f32[48,8,128]{2,1,0:T(8,128)S(1)}) custom-call(s32[3,4,6]{2,1,0:T(4,128)} %bitcast.10, f32[6,8,128,128]{3,2,1,0:T(8,128)} %bitcast.6, bf16[6,8,128,128]{3,2,1,0:T(8,128)(2,1)} %bitcast.7, bf16[6,8,128,128]{3,2,1,0:T(8,128)(2,1)} %bitcast.8, ...), custom_call_target="tpu_custom_call" | custom-call | tf_op jit(solution)/shard_map/exchange/pallas_call | solution.py:515
  12.2 1.7 %finish.1 = f32[6,8,128,128]{3,2,1,0:T(8,128)} custom-call(f32[6,8,128,128]{3,2,1,0:T(8,128)S(1)} %get-tuple-element.8.u, f32[2,128,128]{2,1,0:T(8,128)S(1)} %get-tuple-element.9.cols, f32[48,8,128]{2,1,0:T(8,128)S(1)} %get-tuple-element.10.rows), custom_call_target="tpu_custom_call" | custom-call | tf_op jit(solution)/shard_map/finish/pallas_call | solution.py:550

commit v4 on v3

--- a/solution.py
+++ b/solution.py
@@ -27,7 +27,7 @@
 
 def hubs_of(total, across):
     middle = total // 2
-    return (middle - across - 1, middle - across + 1, middle - across + 3, middle + 1)
+    return (middle - 2 * across + 1, middle - across - 1, middle - across + 1, middle + 1)
 
 
 def edge_tile(edge, spot, across):
@@ -351,32 +351,6 @@
 
     arrive(0)
     compute(0, half)
-
-    @pl.when(deferred)
-    def _():
-        send_neighbours()
-
-    @pl.when(am_hub == 1)
-    def _():
-        pl.semaphore_wait(ready, total - 1)
-        pltpu.make_async_copy(r, r, r_sem).wait()
-        place = jnp.where(me == hubs[1], 1, 0) + jnp.where(me == hubs[2], 2, 0) + jnp.where(me == hubs[3], 3, 0)
-        for owner, parity, e, spot in seams:
-            slot = ((parity * 4 + e) * across + spot) * half
-            for n in range(half):
-                d[slot + n] = r[route[slot + n]]
-            src = d.at[pl.ds(slot, half)]
-            dst = h.at[parity, e, :, place]
-            if owner in hubs:
-                @pl.when(me != owner)
-                def _():
-                    remote(src, dst, send2, h_sem, owner).start()
-
-                @pl.when(me == owner)
-                def _():
-                    pltpu.make_async_copy(src, dst, h_sem).start()
-            else:
-                remote(src, dst, send2, h_sem, owner).start()
 
     arrive(1)
     sub = lax.broadcasted_iota(jnp.int32, (8, 128), 0)
@@ -405,6 +379,32 @@
                 if k > 0:
                     carry[spot] = inverses[k] * below
                 below = jnp.where(inner, packed_columns(coupling_columns, group), packed_rows(coupling, p, k, low))
+
+    @pl.when(deferred)
+    def _():
+        send_neighbours()
+
+    @pl.when(am_hub == 1)
+    def _():
+        pl.semaphore_wait(ready, total - 1)
+        pltpu.make_async_copy(r, r, r_sem).wait()
+        place = jnp.where(me == hubs[1], 1, 0) + jnp.where(me == hubs[2], 2, 0) + jnp.where(me == hubs[3], 3, 0)
+        for owner, parity, e, spot in seams:
+            slot = ((parity * 4 + e) * across + spot) * half
+            for n in range(half):
+                d[slot + n] = r[route[slot + n]]
+            src = d.at[pl.ds(slot, half)]
+            dst = h.at[parity, e, :, place]
+            if owner in hubs:
+                @pl.when(me != owner)
+                def _():
+                    remote(src, dst, send2, h_sem, owner).start()
+
+                @pl.when(me == owner)
+                def _():
+                    pltpu.make_async_copy(src, dst, h_sem).start()
+            else:
+                remote(src, dst, send2, h_sem, owner).start()
 
     compute(half, panels)
 

time: 14 us -> 13.9 us (level)
  no operation moved by 1% of the time
where the time goes in v4:
time: 13.9 us; the launch traced here: 13.8 us
  Pallas kernels  13.8 us (99%)
    pallas_call x1, Pallas kernels, shards(): pl.pallas_call(functools.partial(exchange_kernel, total, across), out_sha...  12 us
    pallas_call x1, Pallas kernels, shards(): pl.pallas_call(finish_kernel, out_shape=jax.ShapeDtypeStruct(shape, jnp.f...  1.75 us

profile of v4, /device:TPU:0, one launch (start us, length us, event | category | flops | bytes accessed | tf_op | source)
XLA Modules:
  0.0 13.8 jit_solution(15651278690763614342)
XLA Ops:
  0.0 12.0 %exchange.1 = (f32[6,8,128,128]{3,2,1,0:T(8,128)S(1)}, f32[2,128,128]{2,1,0:T(8,128)S(1)}, f32[48,8,128]{2,1,0:T(8,128)S(1)}) custom-call(s32[3,4,6]{2,1,0:T(4,128)} %bitcast.10, f32[6,8,128,128]{3,2,1,0:T(8,128)} %bitcast.6, bf16[6,8,128,128]{3,2,1,0:T(8,128)(2,1)} %bitcast.7, bf16[6,8,128,128]{3,2,1,0:T(8,128)(2,1)} %bitcast.8, ...), custom_call_target="tpu_custom_call" | custom-call | tf_op jit(solution)/shard_map/exchange/pallas_call | solution.py:515
  12.0 1.7 %finish.1 = f32[6,8,128,128]{3,2,1,0:T(8,128)} custom-call(f32[6,8,128,128]{3,2,1,0:T(8,128)S(1)} %get-tuple-element.8.u, f32[2,128,128]{2,1,0:T(8,128)S(1)} %get-tuple-element.9.cols, f32[48,8,128]{2,1,0:T(8,128)S(1)} %get-tuple-element.10.rows), custom_call_target="tpu_custom_call" | custom-call | tf_op jit(solution)/shard_map/finish/pallas_call | solution.py:550
